TPU v7x, 32 devices: a whole 2x2x4 slice. The times are simulated.
32 devices in a mesh: grp: 4 (over y, x), dev: 8 (over z, core).
Axes of the slice: x: 2, y: 2, z: 4, core: 2. Of those that a mesh axis runs over, the one named last changes fastest.
Arguments:
- feeder_state: float32 [3072, 24, 256], P(('grp', 'dev')), may hold values from -6 to 6
- feeder_load: bfloat16 [3072, 24, 256], P(('grp', 'dev')), may hold values from -6 to 6
- feeder_inverse: bfloat16 [3072, 256, 256], P(('grp', 'dev')), as said below
- coupling: bfloat16 [3072, 256], P(('grp', 'dev')), may hold values from -0.375 to 0.375
- feeder_bus: int32 [3072], P(('grp', 'dev')), may hold values from 0 to 4095
- bus_coupling: bfloat16 [4096, 4096], P(('grp', 'dev')), may hold values from -0.1875 to 0.1875
- bus_diagonal: float32 [4096], P(('grp', 'dev')), may hold values from 1 to 3
- bus_load: float32 [24, 4096], P(None, ('grp', 'dev')), may hold values from -6 to 6
- bus_state: float32 [24, 4096], P(None, ('grp', 'dev')), may hold values from -6 to 6
- barrier: float32 [2], replicated, may hold values from 0.5 to 4
- step_length: float32 [2], replicated, may hold values from 0.4 to 1
Outputs:
- feeder_final: float32 [3072, 24, 256], P(('grp', 'dev'))
- bus_final: float32 [24, 4096], P(None, ('grp', 'dev'))
Inputs may be any that keep to these rules, and one draw needn't show every extreme that they name: `feeder_inverse`: each block is symmetric with a positive diagonal and is positive definite.
All inputs are finite; a program needn't handle non-finite values.
Results may differ from a plain program's by a relative error of at most 0.0022.
Values may be sent and summed in bfloat16 or wider, within the bound.
No kernel may reach another device: no remote copies, remote signals or barrier semaphores. Data moves between devices by JAX's collectives and lax.ppermute only.
A program may use at most 128 MiB of HBM per device.

v0:
```python
import jax
import jax.numpy as jnp
from jax import lax
from jax.sharding import PartitionSpec as P


def on_device(
    feeder_state,
    feeder_load,
    feeder_inverse,
    coupling,
    feeder_bus,
    bus_coupling,
    bus_diagonal,
    bus_load,
    bus_state,
    barrier,
    step_length,
):
    highest = lax.Precision.HIGHEST
    sensitivity = coupling.astype(jnp.float32)
    response = jnp.einsum(
        "fij,fj->fi", feeder_inverse, coupling, preferred_element_type=jnp.float32
    )
    schur = jnp.sum(sensitivity * response, axis=-1)
    bus_local = bus_coupling.shape[0]
    schur_all, buses_all = (
        lax.all_gather(schur, ("grp", "dev"), axis=0, tiled=True),
        lax.all_gather(feeder_bus.astype(jnp.float32), ("grp", "dev"), axis=0, tiled=True),
    )
    bus_first = lax.axis_index(("grp", "dev")) * bus_local
    owned = (
        buses_all.astype(jnp.int32)[:, None]
        == bus_first + jnp.arange(bus_local, dtype=jnp.int32)[None, :]
    ).astype(jnp.float32)
    bus_schur = jnp.dot(schur_all, owned, precision=highest)
    feeder_now = feeder_state
    bus_now = bus_state
    for iteration in range(barrier.shape[0]):
        weight_mu = barrier[iteration]
        residual = (
            feeder_load.astype(jnp.float32) + weight_mu * jax.nn.sigmoid(-feeder_now)
        ).astype(jnp.bfloat16)
        solved = jnp.einsum(
            "fij,fhj->fhi", feeder_inverse, residual, preferred_element_type=jnp.float32
        )
        boundary = jnp.sum(solved * sensitivity[:, None, :], axis=-1)
        boundary_all = lax.all_gather(boundary.T, ("grp", "dev"), axis=1, tiled=True)
        bus_totals = jnp.dot(boundary_all, owned, precision=highest)
        bus_right = bus_load + weight_mu * jax.nn.sigmoid(-bus_now) - bus_totals
        pivots = bus_diagonal + weight_mu + bus_schur
        first_sweep = (bus_right / pivots).astype(jnp.bfloat16)
        coupled = jnp.einsum(
            "hk,bk->hb",
            lax.all_gather(first_sweep, ("grp", "dev"), axis=1, tiled=True),
            bus_coupling,
            preferred_element_type=jnp.float32,
        )
        second_sweep = (bus_right - coupled) / pivots
        bus_now = bus_now + step_length[iteration] * second_sweep
        all_steps = lax.all_gather(second_sweep, ("grp", "dev"), axis=1, tiled=True)
        at_feeder = jnp.take(all_steps, feeder_bus, axis=1)
        feeder_now = feeder_now + step_length[iteration] * (
            solved - response[:, None, :] * at_feeder.T[:, :, None]
        )
    return (feeder_now, bus_now)


def solution(mesh):
    in_specs = (
        P(("grp", "dev"), None, None),
        P(("grp", "dev"), None, None),
        P(("grp", "dev"), None, None),
        P(("grp", "dev"), None),
        P(("grp", "dev")),
        P(("grp", "dev"), None),
        P(("grp", "dev")),
        P(None, ("grp", "dev")),
        P(None, ("grp", "dev")),
        P(),
        P(),
    )
    out_specs = (P(("grp", "dev"), None, None), P(None, ("grp", "dev")))
    return jax.shard_map(
        on_device, mesh=mesh, in_specs=in_specs, out_specs=out_specs, check_vma=False
    )
```

profile of v0, /device:TPU:1, one launch (start us, length us, event | category | flops | bytes accessed | tf_op | source)
XLA Modules:
  0.0 364.4 jit_solution(17489155133929602478)
XLA Ops:
  0.6 0.0 copy-start
  0.7 0.5 iota_add_fusion
  1.1 1.2 compare_and_fusion
  2.3 0.7 compare_select_fusion
  3.0 1.4 fusion.38
  4.3 1.3 fusion.37
  5.7 0.6 pad_clamp_fusion
  6.3 0.6 broadcast.29.clone
  6.9 1.4 convert_dynamic-update-slice_fusion
  8.2 0.0 copy-start.2
  8.2 0.0 copy-start.1
  8.2 8.1 %fusion.33 = f32[96,1,256]{2,1,0:T(1,128)S(1)} fusion(bf16[96,256,256]{2,1,0:T(8,128)(2,1)} %param.15, bf16[96,256,1]{1,0,2:T(8,128)(2,1)} %bitcast.35), kind=kOutput, calls=%fused_computation.36 | convolution fusion | flops 12582912 | bytes 12730368 | tf_op jit(solution)/shard_map/fij,fj->fi/dot_general | solution.py:22
  16.3 0.0 copy-done.2
  16.3 0.6 multiply_reduce_fusion.2
  16.9 0.6 broadcast.29.clone.1
  17.5 1.4 dynamic-update-slice.1
  19.0 0.7 copy.34
  19.6 41.0 %all-reduce.2 = (f32[3072]{0:T(1024)S(1)}, f32[3072]{0:T(1024)S(1)}) all-reduce(f32[3072]{0:T(1024)} %convert_dynamic-update-slice_fusion, f32[3072]{0:T(1024)} %dynamic-update-slice.1), channel_id=1, replica_groups=mesh['grp'=4,'dev'=8] {'grp','dev'}, use_global_device_ids=true, to_apply=%add | all-reduce | flops 6144 | bytes 49152
  60.6 0.0 copy-start.7
  60.6 3.3 add_add_fusion
  63.9 0.0 copy-start.8
  63.9 0.0 copy-done.1
  63.9 0.0 copy-start.5
  63.9 0.0 copy-start.6
  64.0 0.0 copy-start.9
  64.0 0.0 copy-start.10
  64.0 10.4 %multiply_reduce_fusion.1 = (f32[96,24]{1,0:T(8,128)S(1)}, f32[96,24,256]{2,1,0:T(8,128)}) fusion(f32[96,256]{1,0:T(8,128)S(1)} %convert_element_type.28, bf16[96,256,256]{2,1,0:T(8,128)(2,1)} %param.15, bf16[96,24,256]{2,1,0:T(8,128)(2,1)} %param.14, f32[96,24,256]{2,1,0:T(8,128)S(1)} %copy-done.1, f32[]{:T(128)} %bitcast.1), kind=kOutput, calls=%fused_computation.15 | convolution fusion | flops 306706176 | bytes 18588676 | tf_op jit(solution)/shard_map/fij,fhj->fhi/dot_general | solution.py:44
  74.3 0.0 copy-done.5
  74.3 0.1 copy.21
  74.4 43.2 %all-gather = f32[32,96,24]{1,2,0:T(8,128)S(1)} all-gather(f32[1,96,24]{1,2,0:T(8,128)S(1)} %copy.21), channel_id=1, replica_groups=mesh['grp'=4,'dev'=8] {'grp','dev'}, dimensions={0}, use_global_device_ids=true | all-gather | bytes 304128 | tf_op jit(solution)/shard_map/all_gather | solution.py:48
  117.6 0.8 copy.22
  118.4 1.9 reshape.44
  120.3 0.0 copy-done.7
  120.3 0.0 copy-done.8
  120.3 0.0 copy-done.6
  120.4 0.0 copy-done.9
  120.4 0.0 copy-done.10
  120.4 2.3 divide_convert_fusion.1
  122.7 0.0 copy-start.3
  122.7 37.6 %all_gather.27 = bf16[24,4096]{1,0:T(8,128)(2,1)S(1)} all-gather(bf16[24,128]{1,0:T(8,128)(2,1)S(1)} %get-tuple-element.13), channel_id=1, replica_groups=mesh['grp'=4,'dev'=8] {'grp','dev'}, dimensions={1}, use_global_device_ids=true | all-gather | bytes 202752 | tf_op jit(solution)/shard_map/all_gather | solution.py:55
  160.3 0.0 copy-done
  160.3 1.0 fusion.23
  161.3 0.0 copy-start.4
  161.3 0.6 copy-done.4
  161.9 42.2 %all_gather.28 = f32[24,4096]{1,0:T(8,128)} all-gather(f32[24,128]{1,0:T(8,128)S(1)} %fusion.23), channel_id=1, replica_groups=mesh['grp'=4,'dev'=8] {'grp','dev'}, dimensions={1}, use_global_device_ids=true | all-gather | bytes 405504 | tf_op jit(solution)/shard_map/all_gather | solution.py:61
  204.1 2.9 copy.23
  207.1 2.9 gather_fusion
  210.0 0.9 broadcast_select_fusion.1
  210.9 0.0 copy-done.3
  210.9 13.0 %multiply_reduce_fusion = (f32[96,24]{1,0:T(8,128)}, f32[96,24,256]{2,1,0:T(8,128)}) fusion(f32[96,256]{1,0:T(8,128)} %copy-done.5, bf16[96,256,256]{2,1,0:T(8,128)(2,1)} %param.15, bf16[96,24,256]{2,1,0:T(8,128)(2,1)} %param.14, f32[]{:T(128)} %bitcast.10, f32[96,24,256]{2,1,0:T(8,128)S(1)} %copy-done.1, f32[96,24,256]{2,1,0:T(8,128)} %get-tuple-element.12, ...), kind=kOutput, calls=%fused_computation.13 | convolution fusion | flops 309065472 | bytes 21055496 | tf_op jit(solution)/shard_map/fij,fhj->fhi/dot_general | solution.py:44
  223.8 1.5 copy.24
  225.3 38.7 %all-gather.1 = f32[32,96,24]{1,2,0:T(8,128)S(1)} all-gather(f32[1,96,24]{1,2,0:T(8,128)} %copy.24), channel_id=1, replica_groups=mesh['grp'=4,'dev'=8] {'grp','dev'}, dimensions={0}, use_global_device_ids=true | all-gather | bytes 304128 | tf_op jit(solution)/shard_map/all_gather | solution.py:48
  264.0 0.8 copy.25
  264.9 1.9 reshape.46
  266.8 3.1 divide_convert_fusion
  269.9 38.7 %all_gather.30 = bf16[24,4096]{1,0:T(8,128)(2,1)S(1)} all-gather(bf16[24,128]{1,0:T(8,128)(2,1)S(1)} %get-tuple-element.17), channel_id=1, replica_groups=mesh['grp'=4,'dev'=8] {'grp','dev'}, dimensions={1}, use_global_device_ids=true | all-gather | bytes 202752 | tf_op jit(solution)/shard_map/all_gather | solution.py:55
  308.6 3.0 multiply_add_fusion.3
  311.6 41.1 %all_gather.31 = f32[24,4096]{1,0:T(8,128)} all-gather(f32[24,128]{1,0:T(8,128)S(1)} %get-tuple-element.20), channel_id=1, replica_groups=mesh['grp'=4,'dev'=8] {'grp','dev'}, dimensions={1}, use_global_device_ids=true | all-gather | bytes 405504 | tf_op jit(solution)/shard_map/all_gather | solution.py:61
  352.6 2.9 copy.26
  355.6 2.9 gather_fusion.1
  358.5 0.9 broadcast_select_fusion
  359.4 5.0 %multiply_add_fusion = f32[96,24,256]{2,1,0:T(8,128)} fusion(f32[96,24,256]{2,1,0:T(8,128)} %get-tuple-element.16, f32[96,24]{1,0:T(8,128)S(1)} %broadcast_select_fusion, f32[]{:T(128)} %bitcast.9, f32[96,256]{1,0:T(8,128)S(1)} %bitcast.37, f32[96,24,256]{2,1,0:T(8,128)S(1)} %copy-done.1, f32[96,24,256]{2,1,0:T(8,128)} %get-tuple-element.12, ...), kind=kLoop, calls=%fused_computation.12 | loop fusion | flops 4718592 | bytes 9553928 | tf_op jit(solution)/shard_map/add | solution.py:63
  (2 shorter events, 0.0 us)
Async XLA Ops:
  0.6 159.7 %copy-start = (bf16[128,4096]{1,0:T(8,128)(2,1)S(1)}, bf16[128,4096]{1,0:T(8,128)(2,1)}, u32[]{:S(2)}) copy-start(bf16[128,4096]{1,0:T(8,128)(2,1)} %param.18) | copy-start | bytes 3145732
  8.2 8.1 %copy-start.2 = (bf16[96,256]{1,0:T(8,128)(2,1)S(1)}, bf16[96,256]{1,0:T(8,128)(2,1)}, u32[]{:S(2)}) copy-start(bf16[96,256]{1,0:T(8,128)(2,1)} %param.16) | copy-start | bytes 147460
  8.2 55.7 %copy-start.1 = (f32[96,24,256]{2,1,0:T(8,128)S(1)}, f32[96,24,256]{2,1,0:T(8,128)}, u32[]{:S(2)}) copy-start(f32[96,24,256]{2,1,0:T(8,128)} %param.13) | copy-start | bytes 7077892
  60.6 59.7 %copy-start.7 = (s32[3072]{0:T(1024)}, s32[3072]{0:T(1024)S(1)}, u32[]{:S(2)}) copy-start(s32[3072]{0:T(1024)S(1)} %convert_element_type.30) | copy-start | bytes 36868
  63.9 56.4 %copy-start.8 = (f32[128]{0:T(128)}, f32[128]{0:T(128)S(1)}, u32[]{:S(2)}) copy-start(f32[128]{0:T(128)S(1)} %get-tuple-element.6) | copy-start | bytes 1540
  63.9 10.4 %copy-start.5 = (f32[96,256]{1,0:T(8,128)}, f32[96,256]{1,0:T(8,128)S(1)}, u32[]{:S(2)}) copy-start(f32[96,256]{1,0:T(8,128)S(1)} %convert_element_type.28) | copy-start | bytes 294916
  63.9 56.4 %copy-start.6 = (f32[24,128]{1,0:T(8,128)S(1)}, f32[24,128]{1,0:T(8,128)}, u32[]{:S(2)}) copy-start(f32[24,128]{1,0:T(8,128)} %param.21) | copy-start | bytes 36868
  64.0 56.4 %copy-start.9 = (f32[24,128]{1,0:T(8,128)S(1)}, f32[24,128]{1,0:T(8,128)}, u32[]{:S(2)}) copy-start(f32[24,128]{1,0:T(8,128)} %param.20) | copy-start | bytes 36868
  64.0 56.4 %copy-start.10 = (s32[128]{0:T(128)S(1)}, s32[128]{0:T(128)}, u32[]{:S(2)}) copy-start(s32[128]{0:T(128)} %iota_add_fusion) | copy-start | bytes 1540
  122.7 88.2 %copy-start.3 = (f32[96,1,256]{2,0,1:T(8,128)S(1)}, f32[96,1,256]{2,0,1:T(8,128)}, u32[]{:S(2)}) copy-start(f32[96,1,256]{2,0,1:T(8,128)} %copy.34) | copy-start | bytes 294916
  161.3 0.6 copy-start.4
where the time goes:
time: 366 us; the launch traced here: 364 us
  blocking collectives  282 us (77%)
  matrix products  44.1 us (12%)
  local copies, waits for them, and re-layouts  25.4 us (7%)
  other arithmetic  11.7 us (3%)
    all_gather x2, blocking collectives, on_device(): all_steps = lax.all_gather(second_sweep, ('grp', 'dev'), axis=1, tiled=True)  83.3 us
    all_gather x2, blocking collectives, on_device(): lax.all_gather(boundary.T, ('grp', 'dev'), axis=1, tiled=True)  81.9 us
    all_gather x2, blocking collectives, on_device(): lax.all_gather(first_sweep, ('grp', 'dev'), axis=1, tiled=True)  76.2 us
    unnamed x1, blocking collectives  41 us
    dot_general x2, matrix products, on_device(): jnp.einsum('fij,fhj->fhi', feeder_inverse, residual, preferred_element_ty...  23.3 us
    unnamed x29, local copies, waits for them, and re-layouts  8.69 us
    dot_general x1, matrix products, on_device(): jnp.einsum('fij,fj->fi', feeder_inverse, coupling, preferred_element_type...  8.06 us

commit v1 on v0

v1 whole, which is shorter than its diff:
```python
import functools

import jax
import jax.numpy as jnp
from jax import lax
from jax.experimental import pallas as pl
from jax.experimental.pallas import tpu as pltpu
from jax.sharding import PartitionSpec as P

AXES = ("grp", "dev")
LANES = 128
F32 = jnp.float32
BF16 = jnp.bfloat16


def sigmoid_neg(x):
    return 1.0 / (1.0 + jnp.exp(x))


def split(x):
    high = x.astype(BF16).astype(F32)
    return high, x - high


def lane_iota(rows, lanes=LANES):
    return lax.broadcasted_iota(jnp.int32, (rows, lanes), 1)


def feeder_first(
    block, mu_ref, step_ref, state_ref, load_ref, inverse_ref, coupling_ref, bus_ref,
    diagonal_ref, bus_load_ref, bus_state_ref, partial_ref, response_ref, send_ref, sums_ref, ids_ref,
):
    at = pl.program_id(0)
    hours = state_ref.shape[1]
    mu, step = mu_ref[0], step_ref[0]

    @pl.when(at == 0)
    def _():
        sums_ref[...] = jnp.zeros_like(sums_ref)

    lanes = lane_iota(hours + 8)
    sums = sums_ref[...]
    for k in range(block):
        state = state_ref[k]
        residual = load_ref[k].astype(F32) + mu * sigmoid_neg(state)
        row = jnp.broadcast_to(coupling_ref[pl.ds(k, 1), :].astype(F32), (8, state.shape[1]))
        stacked = jnp.concatenate([residual, row], axis=0).astype(BF16)
        product = jnp.dot(stacked, inverse_ref[k], preferred_element_type=F32)
        response = product[hours : hours + 1]
        partial_ref[k] = state + step * product[:hours]
        response_ref[pl.ds(k, 1), :] = response
        dots = jnp.sum(stacked.astype(F32) * response, axis=1, keepdims=True)
        sums = jnp.where(lanes == at * block + k, dots, sums)
    sums_ref[...] = sums

    @pl.when(at == pl.num_programs(0) - 1)
    def _():
        count = bus_ref.shape[1]
        ids_ref[...] = jnp.full_like(ids_ref, -1)
        ids_ref[0:1, 0:count] = bus_ref[...]
        ids = ids_ref[0:1, :]
        width = 2 * LANES
        schur, schur_low = split(sums_ref[hours : hours + 1, :])
        diag, diag_low = split(diagonal_ref[...])
        rows = lax.broadcasted_iota(jnp.int32, (8, LANES), 0)
        extra = jnp.zeros((8, LANES), F32)
        for at_row, value in enumerate(
            (
                schur,
                schur_low,
                (ids // width).astype(F32),
                (ids % width).astype(F32),
                diag,
                diag_low,
            )
        ):
            extra = jnp.where(rows == at_row, value, extra)
        base = bus_load_ref[...] + mu * sigmoid_neg(bus_state_ref[...])
        message = jnp.concatenate([sums_ref[0:hours, :], extra, base], axis=0).astype(BF16)
        for to in range(send_ref.shape[0]):
            send_ref[to] = message


def digit_columns(ids_ref, first_ref, hours):
    devices = first_ref.shape[0]
    for d in range(devices):
        ids_ref[pl.ds(d, 1), :] = first_ref[d, hours : hours + 8, :].astype(F32)[3:4]
    return ids_ref[...].T


def scatter_buses(totals_ref, ids_ref, first_ref, rows_of, hours):
    digits, height, width = totals_ref.shape
    devices = first_ref.shape[0]
    columns = digit_columns(ids_ref, first_ref, hours)
    low = lax.broadcasted_iota(jnp.int32, (LANES, width), 1).astype(F32)
    for pair in range(devices // 2):
        one_hot, rows, high = [], [], []
        for d in (2 * pair, 2 * pair + 1):
            one_hot.append((columns[:, d : d + 1] == low).astype(F32).astype(BF16))
            rows.append(rows_of(d))
            high.append(first_ref[d, hours : hours + 8, :].astype(F32)[2:3])
        one_hot = jnp.concatenate(one_hot, axis=0)
        rows = jnp.concatenate(rows, axis=1)
        high = jnp.concatenate(high, axis=1)
        picked = jnp.concatenate(
            [jnp.where(high == float(h), rows, 0.0) for h in range(digits)], axis=0
        ).astype(BF16)
        part = jnp.dot(picked, one_hot, preferred_element_type=F32).reshape(digits, height, width)
        if pair == 0:
            totals_ref[...] = part
        else:
            totals_ref[...] += part


def bus_kernel(
    iteration, last, hours, me_ref, mu_ref, step_ref, first_ref, rows_ref, base_ref, bus_coupling_ref,
    diagonal_ref, bus_load_ref, bus_state_ref, schur_in_ref, send_ref, state_out_ref, schur_out_ref,
    totals_ref, ids_ref,
):
    me = me_ref[0]
    mu, step = mu_ref[iteration], step_ref[iteration]
    digits, height, width = totals_ref.shape
    rows_of = lambda d: rows_ref[d, 0:height, :].astype(F32)
    scatter_buses(totals_ref, ids_ref, first_ref, rows_of, hours)
    base_at = base_ref.shape[1] - hours
    coupled = jnp.zeros((hours, bus_coupling_ref.shape[0]), F32)
    for h in range(digits):
        totals = totals_ref[h]
        pair = (2 * h, 2 * h + 1)
        base = jnp.concatenate([base_ref[d, base_at:, :].astype(F32) for d in pair], axis=1)
        extra = jnp.concatenate([first_ref[d, hours : hours + 8, :].astype(F32) for d in pair], axis=1)
        if iteration == 0:
            schur = totals[hours : hours + 1] + totals[hours + 1 : hours + 2]
            schur_out_ref[pl.ds(h, 1), :] = schur
        else:
            schur = schur_in_ref[pl.ds(h, 1), :]
        pivots = extra[4:5] + extra[5:6] + (mu + schur)
        sweep = ((base - totals[:hours]) / pivots).astype(BF16)
        coupled += lax.dot_general(
            sweep,
            bus_coupling_ref[:, h * width : (h + 1) * width],
            (((1,), (1,)), ((), ())),
            preferred_element_type=F32,
        )
    mine = totals_ref[me // 2]
    if iteration == 0:
        schur = mine[hours : hours + 1] + mine[hours + 1 : hours + 2]
    else:
        schur = schur_in_ref[pl.ds(me // 2, 1), :]
    odd = lax.rem(me, 2) == 1
    half = lambda x: jnp.where(odd, x[:, LANES:], x[:, :LANES])
    state = bus_state_ref[...]
    right = bus_load_ref[...] + mu * sigmoid_neg(state) - half(mine)[:hours]
    second = (right - coupled) / (diagonal_ref[...] + mu + half(schur))
    state = state + step * second
    state_out_ref[...] = state
    parts = [second]
    if not last:
        parts.append(bus_load_ref[...] + mu_ref[iteration + 1] * sigmoid_neg(state))
    message = jnp.concatenate(parts, axis=0).astype(BF16)
    for to in range(send_ref.shape[0]):
        send_ref[to] = message


def feeder_middle(
    block, iteration, mu_ref, step_ref, bus_ref, sweep_ref, partial_ref, load_ref, response_ref,
    residual_ref, send_ref, sums_ref,
):
    at = pl.program_id(0)
    hours = load_ref.shape[1]
    mu, step = mu_ref[iteration + 1], step_ref[iteration]

    @pl.when(at == 0)
    def _():
        sums_ref[...] = jnp.zeros_like(sums_ref)

    lanes = lane_iota(hours)
    sums = sums_ref[...]
    for k in range(block):
        bus = bus_ref[at * block + k]
        tile = sweep_ref[bus // LANES, 0:hours, :].astype(F32)
        column = jnp.sum(jnp.where(lanes == bus % LANES, tile, 0.0), axis=1, keepdims=True)
        response = response_ref[pl.ds(k, 1), :]
        state = partial_ref[k] - response * (step * column)
        residual = (load_ref[k].astype(F32) + mu * sigmoid_neg(state)).astype(BF16)
        residual_ref[k] = residual
        dots = jnp.sum(residual.astype(F32) * response, axis=1, keepdims=True)
        sums = jnp.where(lanes == at * block + k, dots, sums)
    sums_ref[...] = sums

    @pl.when(at == pl.num_programs(0) - 1)
    def _():
        message = sums_ref[...].astype(BF16)
        for to in range(send_ref.shape[0]):
            send_ref[to] = message


def feeder_last(
    block, step_ref, bus_ref, first_sweep_ref, second_sweep_ref, partial_ref, residual_ref, inverse_ref,
    response_ref, out_ref,
):
    at = pl.program_id(0)
    hours = partial_ref.shape[1]
    lanes = lane_iota(hours)
    for k in range(block):
        bus = bus_ref[at * block + k]
        tile = step_ref[0] * first_sweep_ref[bus // LANES, 0:hours, :].astype(F32)
        tile += step_ref[1] * second_sweep_ref[bus // LANES, 0:hours, :].astype(F32)
        column = jnp.sum(jnp.where(lanes == bus % LANES, tile, 0.0), axis=1, keepdims=True)
        solved = jnp.dot(residual_ref[k], inverse_ref[k], preferred_element_type=F32)
        out_ref[k] = partial_ref[k] + step_ref[1] * solved - response_ref[pl.ds(k, 1), :] * column


def spread(message):
    return lax.all_to_all(message, AXES, 0, 0, tiled=True)


SMEM = pl.BlockSpec(memory_space=pltpu.SMEM)
VMEM = pl.BlockSpec(memory_space=pltpu.VMEM)
LIMIT = 32 * 1024 * 1024


def on_device(
    devices, feeder_state, feeder_load, feeder_inverse, coupling, feeder_bus, bus_coupling, bus_diagonal,
    bus_load, bus_state, barrier, step_length,
):
    feeders, hours, nodes = feeder_state.shape
    own, buses = bus_coupling.shape
    width = 2 * LANES
    digits = buses // width
    block = 8
    steps = feeders // block
    me = lax.axis_index(AXES).astype(jnp.int32)[None]
    diagonal = bus_diagonal[None, :]
    whole = lambda *shape: pl.BlockSpec(shape, lambda i: (0,) * len(shape))
    cube = pl.BlockSpec((block, hours, nodes), lambda i: (i, 0, 0))
    square = pl.BlockSpec((block, nodes, nodes), lambda i: (i, 0, 0))
    flat = pl.BlockSpec((block, nodes), lambda i: (i, 0))
    params = pltpu.CompilerParams(dimension_semantics=("arbitrary",), vmem_limit_bytes=LIMIT)
    shape = jax.ShapeDtypeStruct

    partial, response, message = pl.pallas_call(
        functools.partial(feeder_first, block),
        grid=(steps,),
        in_specs=[
            SMEM, SMEM, cube, cube, square, flat, whole(1, feeders), whole(1, own), whole(hours, own),
            whole(hours, own),
        ],
        out_specs=[cube, flat, whole(devices, 2 * hours + 8, LANES)],
        out_shape=[
            shape((feeders, hours, nodes), F32),
            shape((feeders, nodes), F32),
            shape((devices, 2 * hours + 8, LANES), BF16),
        ],
        scratch_shapes=[pltpu.VMEM((hours + 8, LANES), F32), pltpu.VMEM((8, LANES), jnp.int32)],
        compiler_params=params,
        name="feeder_first",
    )(
        barrier, step_length, feeder_state, feeder_load, feeder_inverse, coupling, feeder_bus[None, :],
        diagonal, bus_load, bus_state,
    )
    first = spread(message)

    def bus_call(iteration, rows, base, height, state, schur):
        last = iteration == barrier.shape[0] - 1
        out_rows = hours if last else 2 * hours
        return pl.pallas_call(
            functools.partial(bus_kernel, iteration, last, hours),
            in_specs=[SMEM] * 3 + [VMEM] * 8,
            out_specs=[VMEM] * 3,
            out_shape=[
                shape((devices, out_rows, LANES), BF16),
                shape((hours, own), F32),
                shape((digits, width), F32),
            ],
            scratch_shapes=[
                pltpu.VMEM((digits, height, width), F32),
                pltpu.VMEM((devices, LANES), F32),
            ],
            compiler_params=pltpu.CompilerParams(vmem_limit_bytes=(12 + 3 * devices // 10) << 20),
            name=f"bus_sweeps_{iteration}",
        )(me, barrier, step_length, first, rows, base, bus_coupling, diagonal, bus_load, state, schur)

    message, bus_now, schur = bus_call(
        0, first, first, hours + 8, bus_state, jnp.zeros((digits, width), F32)
    )
    sweep_first = spread(message)

    residual, message = pl.pallas_call(
        functools.partial(feeder_middle, block, 0),
        grid=(steps,),
        in_specs=[SMEM, SMEM, SMEM, whole(devices, 2 * hours, LANES), cube, cube, flat],
        out_specs=[cube, whole(devices, hours, LANES)],
        out_shape=[shape((feeders, hours, nodes), BF16), shape((devices, hours, LANES), BF16)],
        scratch_shapes=[pltpu.VMEM((hours, LANES), F32)],
        compiler_params=params,
        name="feeder_middle",
    )(barrier, step_length, feeder_bus, sweep_first, partial, feeder_load, response)
    rows = spread(message)

    message, bus_now, _ = bus_call(1, rows, sweep_first, hours, bus_now, schur)
    sweep_second = spread(message)

    feeder_now = pl.pallas_call(
        functools.partial(feeder_last, block),
        grid=(steps,),
        in_specs=[
            SMEM, SMEM, whole(devices, 2 * hours, LANES), whole(devices, hours, LANES), cube, cube, square,
            flat,
        ],
        out_specs=cube,
        out_shape=shape((feeders, hours, nodes), F32),
        compiler_params=params,
        name="feeder_last",
    )(step_length, feeder_bus, sweep_first, sweep_second, partial, residual, feeder_inverse, response)
    return feeder_now, bus_now


def solution(mesh):
    devices = mesh.shape["grp"] * mesh.shape["dev"]
    in_specs = (
        P(AXES, None, None),
        P(AXES, None, None),
        P(AXES, None, None),
        P(AXES, None),
        P(AXES),
        P(AXES, None),
        P(AXES),
        P(None, AXES),
        P(None, AXES),
        P(),
        P(),
    )
    out_specs = (P(AXES, None, None), P(None, AXES))
    return jax.shard_map(
        functools.partial(on_device, devices), mesh=mesh, in_specs=in_specs, out_specs=out_specs,
        check_vma=False,
    )
```

time: 366 us -> 102 us (0.28)
  blocking collectives: 282 us -> 38.3 us
  matrix products: 44.1 us -> 0 us
  Pallas kernels: 0 us -> 22.4 us
  waiting for transfers between devices: 0 us -> 14.7 us
  other arithmetic: 11.7 us -> 0 us
  local copies, waits for them, and re-layouts: 25.4 us -> 18.3 us
  starting transfers between devices: 0 us -> 7.08 us
    all_gather x6 -> x0, blocking collectives: 241 us -> none  [the longest x2 83.3 us: on_device(): all_steps = lax.all_gather(second_sweep, ('grp', 'dev'), axis=1, tiled=True)]
    dot_general x8 -> x0, matrix products: 44.1 us -> none  [the longest x2 23.3 us: on_device(): jnp.einsum('fij,fhj->fhi', feeder_inverse, residual, preferred_element_ty...]
    unnamed x1 -> x0, blocking collectives: 41 us -> none
    all_to_all x0 -> x3, blocking collectives: none -> 38.3 us  [spread(): return lax.all_to_all(message, AXES, 0, 0, tiled=True)]
    pallas_call x0 -> x5, Pallas kernels: none -> 22.4 us  [the longest x1 6.74 us: on_device(): pl.pallas_call(functools.partial(feeder_last, block), grid=(steps,), in_s...]
    all_to_all x0 -> x1, waiting for transfers between devices: none -> 14.7 us  [spread(): return lax.all_to_all(message, AXES, 0, 0, tiled=True)]
    unnamed x29 -> x40, local copies, waits for them, and re-layouts: 8.69 us -> 18.2 us
    all_gather x4 -> x0, local copies, waits for them, and re-layouts: 7.5 us -> none  [the longest x2 5.86 us: on_device(): all_steps = lax.all_gather(second_sweep, ('grp', 'dev'), axis=1, tiled=True)]
  transfers between devices with their start and end apart: 0 -> 1, of which waited for: 0 -> 1; matrix products, arithmetic and copies ran while one was open for 0% -> 0% of each run, Pallas kernels for 0% -> 0%
where the time goes in v1:
time: 102 us; the launch traced here: 101 us
  blocking collectives  38.3 us (38%)
  Pallas kernels  22.4 us (22%)
  local copies, waits for them, and re-layouts  18.3 us (18%)
  waiting for transfers between devices  14.7 us (14%)
  starting transfers between devices  7.08 us (7%)
    all_to_all x3, blocking collectives, spread(): return lax.all_to_all(message, AXES, 0, 0, tiled=True)  38.3 us
    unnamed x40, local copies, waits for them, and re-layouts  18.2 us
    all_to_all x1, waiting for transfers between devices, spread(): return lax.all_to_all(message, AXES, 0, 0, tiled=True)  14.7 us
    all_to_all x1, starting transfers between devices, spread(): return lax.all_to_all(message, AXES, 0, 0, tiled=True)  7.08 us
    pallas_call x1, Pallas kernels, on_device(): pl.pallas_call(functools.partial(feeder_last, block), grid=(steps,), in_s...  6.74 us
    pallas_call x2, Pallas kernels, bus_call(): pl.pallas_call(functools.partial(bus_kernel, iteration, last, hours), in_...  6.04 us
    pallas_call x1, Pallas kernels, on_device(): pl.pallas_call(functools.partial(feeder_first, block), grid=(steps,), in_...  5.76 us
    pallas_call x1, Pallas kernels, on_device(): pl.pallas_call(functools.partial(feeder_middle, block, 0), grid=(steps,),...  3.86 us
  transfers between devices with their start and end apart: 1, of which 1 were waited for; matrix products, arithmetic and copies ran while one was open for 0% of the time, Pallas kernels for 0%

profile of v1, /device:TPU:1, one launch (start us, length us, event | category | flops | bytes accessed | tf_op | source)
XLA Modules:
  0.0 101.4 jit_solution(10411434525439909937)
XLA Ops:
  0.6 0.0 copy-start
  0.6 4.6 %copy-done = bf16[96,256,256]{2,1,0:T(8,128)(2,1)S(1)} copy-done((bf16[96,256,256]{2,1,0:T(8,128)(2,1)S(1)}, bf16[96,256,256]{2,1,0:T(8,128)(2,1)}, u32[]{:S(2)}) %copy-start) | copy-done | bytes 12582936
  5.2 0.0 copy-start.2
  5.2 1.3 %copy-done.2 = bf16[96,24,256]{2,1,0:T(8,128)(2,1)S(1)} copy-done((bf16[96,24,256]{2,1,0:T(8,128)(2,1)S(1)}, bf16[96,24,256]{2,1,0:T(8,128)(2,1)}, u32[]{:S(2)}) %copy-start.2) | copy-done | bytes 1179672
  6.5 0.0 copy-start.6
  6.5 1.7 %copy-done.6 = f32[96,24,256]{2,1,0:T(8,128)S(1)} copy-done((f32[96,24,256]{2,1,0:T(8,128)S(1)}, f32[96,24,256]{2,1,0:T(8,128)}, u32[]{:S(2)}) %copy-start.6) | copy-done | bytes 2359320
  8.1 0.0 copy-start.7
  8.2 0.7 copy-done.7
  8.9 0.0 copy-start.9
  8.9 0.8 copy-done.9
  9.7 0.0 copy-start.10
  9.7 0.7 copy-done.10
  10.4 0.0 copy-start.12
  10.4 0.7 copy-done.12
  11.0 0.0 copy-start.14
  11.0 0.7 copy-done.14
  11.7 0.0 copy-start.16
  11.7 0.7 copy-done.16
  12.3 0.0 copy-start.18
  12.3 0.7 copy-done.18
  13.0 0.0 copy-start.8
  13.0 0.0 copy-start.11
  13.0 0.0 copy-start.13
  13.0 0.0 copy-start.15
  13.0 0.0 copy-start.19
  13.0 5.8 %feeder_first.1 = (f32[96,24,256]{2,1,0:T(8,128)S(1)}, f32[96,256]{1,0:T(8,128)S(1)}, bf16[32,56,128]{2,1,0:T(8,128)(2,1)}) custom-call(f32[2]{0:T(128)S(1)} %copy-done.14, f32[2]{0:T(128)S(1)} %copy-done.12, f32[96,24,256]{2,1,0:T(8,128)S(1)} %copy-done.6, bf16[96,24,256]{2,1,0:T(8,128)(2,1)S(1)} %copy-done.2, bf16[96,256,256]{2,1,0:T(8,128)(2,1)S(1)} %copy-done, ...), custom_call_target="tpu_custom_call" | custom-call | tf_op jit(solution)/shard_map/feeder_first/pallas_call | solution.py:242
  18.8 0.0 copy-start.17
  18.8 7.1 %all-to-all-start = ((bf16[32,56,128]{2,1,0:T(8,128)(2,1)}), bf16[32,56,128]{2,1,0:T(8,128)(2,1)S(1)}, u32[]{:S(2)}, u32[]{:S(2)}) async-start(bf16[32,56,128]{2,1,0:T(8,128)(2,1)} %get-tuple-element.12), calls=%async_computation | async-start | bytes 917504 | tf_op jit(solution)/shard_map/all_to_all | solution.py:215
  25.9 14.7 %all-to-all-done.first_ref.rows_ref.base_ref = bf16[32,56,128]{2,1,0:T(8,128)(2,1)S(1)} async-done(((bf16[32,56,128]{2,1,0:T(8,128)(2,1)}), bf16[32,56,128]{2,1,0:T(8,128)(2,1)S(1)}, u32[]{:S(2)}, u32[]{:S(2)}) %all-to-all-start) | async-done | bytes 458784 | tf_op jit(solution)/shard_map/all_to_all | solution.py:215
  40.6 0.0 copy-start.3
  40.6 0.0 copy-done.8
  40.6 0.0 copy-done.11
  40.6 0.0 copy-done.13
  40.6 0.0 copy-done.15
  40.6 0.0 copy-done.19
  40.6 0.0 copy-start.4
  40.6 1.3 %copy-done.4 = bf16[128,4096]{1,0:T(8,128)(2,1)S(1)} copy-done((bf16[128,4096]{1,0:T(8,128)(2,1)S(1)}, bf16[128,4096]{1,0:T(8,128)(2,1)}, u32[]{:S(2)}) %copy-start.4) | copy-done | bytes 1048600
  41.9 2.8 %bus_sweeps_0.1 = (bf16[32,48,128]{2,1,0:T(8,128)(2,1)S(1)}, f32[24,128]{1,0:T(8,128)S(1)}, f32[16,256]{1,0:T(8,128)S(1)}) custom-call(s32[1]{0:T(128)} %bitcast.me_ref, f32[2]{0:T(128)S(1)} %copy-done.15, f32[2]{0:T(128)S(1)} %copy-done.13, bf16[32,56,128]{2,1,0:T(8,128)(2,1)S(1)} %all-to-all-done.first_ref.rows_ref.base_ref, ...), custom_call_target="tpu_custom_call" | custom-call | tf_op jit(solution)/shard_map/bus_sweeps_0/pallas_call | solution.py:267
  44.7 15.5 %all_to_all.20.sweep_ref.base_ref.first_sweep_ref = bf16[32,48,128]{2,1,0:T(8,128)(2,1)S(1)} all-to-all(bf16[32,48,128]{2,1,0:T(8,128)(2,1)S(1)} %get-tuple-element.13), channel_id=1, replica_groups=mesh['grp'=4,'dev'=8] {'grp','dev'}, dimensions={0} | all-to-all | bytes 786432 | tf_op jit(solution)/shard_map/all_to_all | solution.py:215
  60.2 0.0 copy-start.5
  60.2 0.0 copy-done.17
  60.2 0.0 copy-done.3
  60.3 3.9 %feeder_middle.1 = (bf16[96,24,256]{2,1,0:T(8,128)(2,1)S(1)}, bf16[32,24,128]{2,1,0:T(8,128)(2,1)S(1)}) custom-call(f32[2]{0:T(128)S(1)} %copy-done.15, f32[2]{0:T(128)S(1)} %copy-done.13, s32[96]{0:T(128)S(1)} %copy-done.17, bf16[32,48,128]{2,1,0:T(8,128)(2,1)S(1)} %all_to_all.20.sweep_ref.base_ref.first_sweep_ref, ...), custom_call_target="tpu_custom_call" | custom-call | tf_op jit(solution)/shard_map/feeder_middle/pallas_call | solution.py:289
  64.1 11.5 %all_to_all.21.rows_ref = bf16[32,24,128]{2,1,0:T(8,128)(2,1)S(1)} all-to-all(bf16[32,24,128]{2,1,0:T(8,128)(2,1)S(1)} %get-tuple-element.16), channel_id=1, replica_groups=mesh['grp'=4,'dev'=8] {'grp','dev'}, dimensions={0} | all-to-all | bytes 393216 | tf_op jit(solution)/shard_map/all_to_all | solution.py:215
  75.6 0.0 copy-done.5
  75.6 3.2 %bus_sweeps_1.1 = (bf16[32,24,128]{2,1,0:T(8,128)(2,1)S(1)}, f32[24,128]{1,0:T(8,128)}, f32[16,256]{1,0:T(8,128)}) custom-call(s32[1]{0:T(128)} %bitcast.me_ref, f32[2]{0:T(128)S(1)} %copy-done.15, f32[2]{0:T(128)S(1)} %copy-done.13, bf16[32,56,128]{2,1,0:T(8,128)(2,1)S(1)} %all-to-all-done.first_ref.rows_ref.base_ref, ...), custom_call_target="tpu_custom_call" | custom-call | tf_op jit(solution)/shard_map/bus_sweeps_1/pallas_call | solution.py:267
  78.9 11.2 %all_to_all.22.second_sweep_ref = bf16[32,24,128]{2,1,0:T(8,128)(2,1)S(1)} all-to-all(bf16[32,24,128]{2,1,0:T(8,128)(2,1)S(1)} %get-tuple-element.19), channel_id=1, replica_groups=mesh['grp'=4,'dev'=8] {'grp','dev'}, dimensions={0} | all-to-all | bytes 393216 | tf_op jit(solution)/shard_map/all_to_all | solution.py:215
  90.1 0.0 copy-start.1
  90.1 4.6 %copy-done.1 = bf16[96,256,256]{2,1,0:T(8,128)(2,1)S(1)} copy-done((bf16[96,256,256]{2,1,0:T(8,128)(2,1)S(1)}, bf16[96,256,256]{2,1,0:T(8,128)(2,1)}, u32[]{:S(2)}) %copy-start.1) | copy-done | bytes 12582936
  94.7 6.7 %feeder_last.1 = f32[96,24,256]{2,1,0:T(8,128)} custom-call(f32[2]{0:T(128)S(1)} %copy-done.13, s32[96]{0:T(128)S(1)} %copy-done.17, bf16[32,48,128]{2,1,0:T(8,128)(2,1)S(1)} %all_to_all.20.sweep_ref.base_ref.first_sweep_ref, bf16[32,24,128]{2,1,0:T(8,128)(2,1)S(1)} %all_to_all.22.second_sweep_ref, f32[96,24,256]{2,1,0:T(8,128)S(1)} %get-tuple-element.14.partial_ref, ...), custom_call_target="tpu_custom_call" | custom-call | tf_op jit(solution)/shard_map/feeder_last/pallas_call | solution.py:304
  (1 shorter events, 0.0 us)
Async XLA Ops:
  0.6 4.6 %copy-start = (bf16[96,256,256]{2,1,0:T(8,128)(2,1)S(1)}, bf16[96,256,256]{2,1,0:T(8,128)(2,1)}, u32[]{:S(2)}) copy-start(bf16[96,256,256]{2,1,0:T(8,128)(2,1)} %inverse_ref.3) | copy-start | bytes 37748740
  5.2 1.3 %copy-start.2 = (bf16[96,24,256]{2,1,0:T(8,128)(2,1)S(1)}, bf16[96,24,256]{2,1,0:T(8,128)(2,1)}, u32[]{:S(2)}) copy-start(bf16[96,24,256]{2,1,0:T(8,128)(2,1)} %load_ref.3) | copy-start | bytes 3538948
  6.5 1.7 %copy-start.6 = (f32[96,24,256]{2,1,0:T(8,128)S(1)}, f32[96,24,256]{2,1,0:T(8,128)}, u32[]{:S(2)}) copy-start(f32[96,24,256]{2,1,0:T(8,128)} %state_ref.1) | copy-start | bytes 7077892
  8.1 0.7 copy-start.7
  8.9 0.8 copy-start.9
  9.7 0.7 copy-start.10
  10.4 0.7 copy-start.12
  11.0 0.7 copy-start.14
  11.7 0.7 copy-start.16
  12.3 0.7 copy-start.18
  13.0 27.6 %copy-start.8 = (f32[24,128]{1,0:T(8,128)S(1)}, f32[24,128]{1,0:T(8,128)}, u32[]{:S(2)}) copy-start(f32[24,128]{1,0:T(8,128)} %bus_load_ref.5) | copy-start | bytes 36868
  13.0 27.6 %copy-start.11 = (f32[24,128]{1,0:T(8,128)S(1)}, f32[24,128]{1,0:T(8,128)}, u32[]{:S(2)}) copy-start(f32[24,128]{1,0:T(8,128)} %bus_state_ref.3) | copy-start | bytes 36868
  13.0 27.6 %copy-start.13 = (f32[2]{0:T(128)S(1)}, f32[2]{0:T(128)}, u32[]{:S(2)}) copy-start(f32[2]{0:T(128)} %step_ref.9) | copy-start | bytes 28
  13.0 27.6 %copy-start.15 = (f32[2]{0:T(128)S(1)}, f32[2]{0:T(128)}, u32[]{:S(2)}) copy-start(f32[2]{0:T(128)} %mu_ref.7) | copy-start | bytes 28
  13.0 27.6 %copy-start.19 = (f32[128]{0:T(128)S(1)}, f32[128]{0:T(128)}, u32[]{:S(2)}) copy-start(f32[128]{0:T(128)} %param.17) | copy-start | bytes 1540
  18.8 41.5 %copy-start.17 = (s32[96]{0:T(128)S(1)}, s32[96]{0:T(128)}, u32[]{:S(2)}) copy-start(s32[96]{0:T(128)} %bus_ref.3) | copy-start | bytes 1156
  18.8 21.8 %all-to-all-start = ((bf16[32,56,128]{2,1,0:T(8,128)(2,1)}), bf16[32,56,128]{2,1,0:T(8,128)(2,1)S(1)}, u32[]{:S(2)}, u32[]{:S(2)}) async-start(bf16[32,56,128]{2,1,0:T(8,128)(2,1)} %get-tuple-element.12), calls=%async_computation | async-start | bytes 917504 | tf_op jit(solution)/shard_map/all_to_all | solution.py:215
  40.6 19.7 %copy-start.3 = (bf16[96,24,256]{2,1,0:T(8,128)(2,1)S(1)}, bf16[96,24,256]{2,1,0:T(8,128)(2,1)}, u32[]{:S(2)}) copy-start(bf16[96,24,256]{2,1,0:T(8,128)(2,1)} %load_ref.3) | copy-start | bytes 3538948
  40.6 1.3 %copy-start.4 = (bf16[128,4096]{1,0:T(8,128)(2,1)S(1)}, bf16[128,4096]{1,0:T(8,128)(2,1)}, u32[]{:S(2)}) copy-start(bf16[128,4096]{1,0:T(8,128)(2,1)} %bus_coupling_ref.3) | copy-start | bytes 3145732
  60.2 15.4 %copy-start.5 = (bf16[128,4096]{1,0:T(8,128)(2,1)S(1)}, bf16[128,4096]{1,0:T(8,128)(2,1)}, u32[]{:S(2)}) copy-start(bf16[128,4096]{1,0:T(8,128)(2,1)} %bus_coupling_ref.3) | copy-start | bytes 3145732
  90.1 4.6 %copy-start.1 = (bf16[96,256,256]{2,1,0:T(8,128)(2,1)S(1)}, bf16[96,256,256]{2,1,0:T(8,128)(2,1)}, u32[]{:S(2)}) copy-start(bf16[96,256,256]{2,1,0:T(8,128)(2,1)} %inverse_ref.3) | copy-start | bytes 37748740
